TPU v7x, 32 devices: a whole 2x2x4 slice. The times are simulated.
32 devices in a mesh: groups: 2 (over y), row: 4 (over z), col: 2 (over x), sub: 2 (over core).
Axes of the slice: x: 2, y: 2, z: 4, core: 2. Of those that a mesh axis runs over, the one named last changes fastest.
Arguments:
- matrix: float32 [16384, 8192], P(('groups', 'row'), ('col', 'sub')), parts along dimension 0, may hold values from -60 to 60
- basis_vectors: float32 [16384, 1024], P(('groups', 'row'), ('col', 'sub')), parts along dimension 0, may hold values from -0.0625 to 0.0625
- split_size: int32 [2], P('groups'), parts along dimension 0, may hold values from 256 to 767
Outputs:
- children: float32 [2, 2048, 1024], P('sub', ('groups', 'row'), 'col'), parts along dimension 1
There are 2 independent parts, one for each index of `groups`. A program takes and returns all parts, laid end to end along the dimension named above; each array names one. Nothing has to cross between parts.
Inputs may be any that keep to these rules, and one draw needn't show every extreme that they name: The second subspace has 1024 minus split_size vectors.
All inputs are finite; a program needn't handle non-finite values.
Results may differ from a plain program's by a relative error of at most 0.00011.
Values sent between devices are 32-bit elements; how exact they have to be, the bound alone decides.
A program may use at most 128 MiB of HBM per device.

v0:
```python
import jax
import jax.numpy as jnp
from jax import lax
from jax.sharding import PartitionSpec as P


def shards(matrix, basis_vectors, split_size):
    strip = lax.all_gather(basis_vectors, "row", axis=0, tiled=True)
    row_panel = lax.all_to_all(strip, ("col", "sub"), split_axis=0, concat_axis=1, tiled=True)
    partial_image = jnp.dot(
        matrix, row_panel, precision=lax.Precision.HIGHEST, preferred_element_type=jnp.float32
    )
    image = lax.psum_scatter(partial_image, ("col", "sub"), scatter_dimension=1, tiled=True)
    partial_proj = lax.dot_general(
        lax.all_gather(basis_vectors, ("col", "sub"), axis=1, tiled=True),
        image,
        (((0,), (0,)), ((), ())),
        precision=lax.Precision.HIGHEST,
        preferred_element_type=jnp.float32,
    )
    proj_block = lax.psum_scatter(partial_proj, "row", scatter_dimension=0, tiled=True)
    child_block = lax.all_gather(proj_block, "sub", axis=1, tiled=True)
    row_ids = (
        jnp.arange(child_block.shape[0], dtype=jnp.int32)
        + lax.axis_index("row") * child_block.shape[0]
    )
    col_ids = (
        jnp.arange(child_block.shape[1], dtype=jnp.int32)
        + lax.axis_index("col") * child_block.shape[1]
    )
    leading = split_size[0]
    row_first = row_ids < leading
    col_first = col_ids < leading
    mask_one = row_first[:, None] & col_first[None, :]
    mask_two = jnp.logical_not(row_first)[:, None] & jnp.logical_not(col_first)[None, :]
    selected = jnp.where(lax.axis_index("sub") == 0, mask_one, mask_two)
    return jnp.where(selected, child_block, jnp.zeros((), jnp.float32))[None]


def solution(mesh):
    placed = (
        P(("groups", "row"), ("col", "sub")),
        P(("groups", "row"), ("col", "sub")),
        P("groups"),
    )
    return jax.shard_map(
        shards,
        mesh=mesh,
        in_specs=placed,
        out_specs=P("sub", ("groups", "row"), "col"),
        check_vma=False,
    )
```

profile of v0, /device:TPU:0, one launch (start us, length us, event | category | flops | bytes accessed | tf_op | source)
XLA Modules:
  0.0 493.2 jit_solution(18207130917740719552)
XLA Ops:
  6.5 0.0 all-gather.3.cloned.1.call-start
  6.5 0.7 all-gather.3.cloned.1.call-update
  7.3 0.0 all-gather.5.cloned.1.call-start
  7.3 0.7 all-gather.5.cloned.1.call-update
  8.0 0.0 reduce-scatter.3.cloned.1.call-start
  8.1 153.2 %all-gather.3.cloned.1.call-done = f32[8192,256]{1,0:T(8,128)} async-done(((f32[2048,256]{1,0:T(8,128)}), f32[8192,256]{1,0:T(8,128)}) %all-gather.3.cloned.1.call-update) | async-done | bytes 8388624 | tf_op jit(solution)/shard_map/all_gather | solution.py:8
  161.3 145.5 %all_to_all.19 = f32[4,2048,256]{2,1,0:T(8,128)} all-to-all(f32[4,2048,256]{2,1,0:T(8,128)} %bitcast.15), channel_id=1, replica_groups=mesh['groups'=2,'row'=4,'col'=2,'sub'=2] {'col','sub'}, dimensions={0} | all-to-all | bytes 16777216 | tf_op jit(solution)/shard_map/all_to_all | solution.py:9
  306.7 8.8 %copy.6 = f32[2048,4,256]{0,2,1:T(8,128)} copy(f32[2048,4,256]{2,0,1:T(8,128)} %bitcast.14) | data formatting | bytes 16777216 | tf_op jit(solution)/shard_map/all_to_all | solution.py:9
  315.5 60.4 %fusion.2 = f32[2048,1024]{1,0:T(8,128)} fusion(f32[2048,2048]{1,0:T(8,128)} %param.3, f32[2048,1024]{0,1:T(8,128)} %bitcast.16), kind=kOutput, calls=%fused_computation.6 | convolution fusion | flops 51539607552 | bytes 33554432 | tf_op jit(solution)/shard_map/dot_general | solution.py:10
  376.0 0.0 reduce-scatter.3.cloned.1.call-update
  376.0 0.2 reduce-scatter.5.cloned.1.call-start
  376.2 0.0 all-gather.5.cloned.1.call-done
  376.2 68.4 %reduce-scatter.3.cloned.1.call-done = f32[2048,256]{1,0:T(8,128)} async-done(((f32[2048,1024]{1,0:T(8,128)}), f32[2048,256]{1,0:T(8,128)}) %reduce-scatter.3.cloned.1.call-update) | async-done | bytes 2097168 | tf_op jit(solution)/shard_map/reduce_scatter | solution.py:13
  444.6 11.0 %convolution_bitcast_fusion = f32[1024,256]{0,1:T(8,128)} fusion(f32[2048,256]{1,0:T(8,128)} %reduce-scatter.3.cloned.1.call-done, f32[2048,1024]{1,0:T(8,128)} %all-gather.5.cloned.1.call-done), kind=kOutput, calls=%fused_computation | convolution fusion | flops 6442450944 | bytes 11534336 | tf_op jit(solution)/shard_map/dot_general | solution.py:14
  455.6 0.0 reduce-scatter.5.cloned.1.call-update
  456.3 26.8 %reduce-scatter.5.cloned.1.call-done = f32[256,256]{0,1:T(8,128)} async-done(((f32[1024,256]{0,1:T(8,128)}), f32[256,256]{0,1:T(8,128)}) %reduce-scatter.5.cloned.1.call-update) | async-done | bytes 262160 | tf_op jit(solution)/shard_map/reduce_scatter | solution.py:21
  483.1 2.4 all_gather.11
  485.5 0.2 select_bitcast_fusion
  485.7 1.0 copy.7
  (2 shorter events, 0.0 us)
Async XLA Ops:
  6.5 154.7 %all-gather.3.cloned.1.call-start = ((), (), s32[]{:S(2)}) async-start(), calls=%async_computation.3 | async-start | bytes 10485760 | tf_op jit(solution)/shard_map/all_gather | solution.py:8
  7.3 369.0 %all-gather.5.cloned.1.call-start = ((), (), s32[]{:S(2)}) async-start(), calls=%async_computation.5 | async-start | bytes 10485760 | tf_op jit(solution)/shard_map/all_gather | solution.py:15
  8.0 436.6 %reduce-scatter.3.cloned.1.call-start = ((), (), s32[]{:S(2)}) async-start(), calls=%async_computation.4 | async-start | bytes 10485760 | tf_op jit(solution)/shard_map/reduce_scatter | solution.py:13
  376.0 107.1 %reduce-scatter.5.cloned.1.call-start = ((), (), s32[]{:S(2)}) async-start(), calls=%async_computation.6 | async-start | bytes 1310720 | tf_op jit(solution)/shard_map/reduce_scatter | solution.py:21
Sparse Core Ops, SparseCore 0:
  8.9 152.3 all-gather.2
  162.8 101.4 all-gather.4
  376.1 68.5 reduce-scatter.2
  455.8 27.2 reduce-scatter.4
where the time goes:
time: 494 us; the launch traced here: 493 us
  waiting for transfers between devices  250 us (51%)
  blocking collectives  148 us (30%)
  matrix products  71.4 us (14%)
  between operations  13.8 us (3%)
  local copies, waits for them, and re-layouts  9.76 us (2%)
    all_gather x1, waiting for transfers between devices, shards(): strip = lax.all_gather(basis_vectors, 'row', axis=0, tiled=True)  153 us
    all_to_all x1, blocking collectives, shards(): lax.all_to_all(strip, ('col', 'sub'), split_axis=0, concat_axis=1, tiled=...  145 us
    reduce_scatter x1, waiting for transfers between devices, shards(): lax.psum_scatter(partial_image, ('col', 'sub'), scatter_dimension=1, tile...  68.4 us
    dot_general x1, matrix products, shards(): jnp.dot(matrix, row_panel, precision=lax.Precision.HIGHEST, preferred_ele...  60.4 us
    reduce_scatter x1, waiting for transfers between devices, shards(): lax.psum_scatter(partial_proj, 'row', scatter_dimension=0, tiled=True)  26.8 us
    dot_general x1, matrix products, shards(): lax.dot_general(lax.all_gather(basis_vectors, ('col', 'sub'), axis=1, til...  11 us
  transfers between devices with their start and end apart: 4, of which 3 were waited for; matrix products, arithmetic and copies ran while one was open for 14% of the time, Pallas kernels for 0%

commit v1 on v0

--- a/solution.py
+++ b/solution.py
@@ -5,21 +5,36 @@
 
 
 def shards(matrix, basis_vectors, split_size):
-    strip = lax.all_gather(basis_vectors, "row", axis=0, tiled=True)
-    row_panel = lax.all_to_all(strip, ("col", "sub"), split_axis=0, concat_axis=1, tiled=True)
-    partial_image = jnp.dot(
-        matrix, row_panel, precision=lax.Precision.HIGHEST, preferred_element_type=jnp.float32
+    R = lax.axis_size("row")
+    S = lax.axis_size("sub")
+    C = lax.axis_size("col") * S
+    m, kd = basis_vectors.shape
+    K = kd * C
+    n = matrix.shape[1]
+    per = n // m
+    piece = m // R
+    spread = lax.all_to_all(basis_vectors, "row", split_axis=0, concat_axis=0, tiled=True)
+    mine = lax.all_to_all(spread, ("col", "sub"), split_axis=0, concat_axis=1, tiled=True)
+    own = lax.all_gather(basis_vectors, ("col", "sub"), axis=1, tiled=True)
+    part = lax.dot_general(
+        matrix,
+        own,
+        (((0,), (0,)), ((), ())),
+        precision=lax.Precision.HIGH,
+        preferred_element_type=jnp.float32,
     )
-    image = lax.psum_scatter(partial_image, ("col", "sub"), scatter_dimension=1, tiled=True)
+    part = part.reshape(per, R, piece, K).transpose(1, 0, 2, 3).reshape(R * per * piece, K)
+    image = lax.psum_scatter(part, "row", scatter_dimension=0, tiled=True)
     partial_proj = lax.dot_general(
-        lax.all_gather(basis_vectors, ("col", "sub"), axis=1, tiled=True),
+        mine,
         image,
         (((0,), (0,)), ((), ())),
-        precision=lax.Precision.HIGHEST,
+        precision=lax.Precision.HIGH,
         preferred_element_type=jnp.float32,
     )
-    proj_block = lax.psum_scatter(partial_proj, "row", scatter_dimension=0, tiled=True)
-    child_block = lax.all_gather(proj_block, "sub", axis=1, tiled=True)
+    proj = lax.psum_scatter(partial_proj, "row", scatter_dimension=0, tiled=True)
+    proj = lax.psum_scatter(proj, ("col", "sub"), scatter_dimension=1, tiled=True)
+    child_block = lax.all_gather(proj, "sub", axis=1, tiled=True)
     row_ids = (
         jnp.arange(child_block.shape[0], dtype=jnp.int32)
         + lax.axis_index("row") * child_block.shape[0]

time: 494 us -> 417 us (0.84)
  waiting for transfers between devices: 250 us -> 214 us
  matrix products: 71.4 us -> 44.3 us
  blocking collectives: 148 us -> 140 us
  local copies, waits for them, and re-layouts: 9.76 us -> 4.35 us
    all_gather x2 -> x1, waiting for transfers between devices: 153 us -> 62.6 us  [shards(): own = lax.all_gather(basis_vectors, ('col', 'sub'), axis=1, tiled=True)]
    reduce_scatter x1, waiting for transfers between devices: 26.8 us -> 81.6 us  [shards(): lax.psum_scatter(partial_proj, 'row', scatter_dimension=0, tiled=True)]
    dot_general x2, matrix products: 71.4 us -> 44.3 us  [the longest x1 33.4 us: shards(): lax.dot_general(matrix, own, (((0,), (0,)), ((), ())), precision=lax.Prec...]
    all_to_all x1 -> x2, blocking collectives: 145 us -> 137 us  [the longest x1 109 us: shards(): lax.all_to_all(basis_vectors, 'row', split_axis=0, concat_axis=0, tiled=T...]
    all_to_all x1, local copies, waits for them, and re-layouts: 8.76 us -> 1.84 us  [shards(): lax.all_to_all(spread, ('col', 'sub'), split_axis=0, concat_axis=1, tiled...]
    reduce_scatter x1 -> x2, waiting for transfers between devices: 68.4 us -> 69.5 us  [the longest x1 42.5 us: shards(): image = lax.psum_scatter(part, 'row', scatter_dimension=0, tiled=True)]
  transfers between devices with their start and end apart: 4 -> 4, of which waited for: 3 -> 4; matrix products, arithmetic and copies ran while one was open for 14% -> 0% of each run, Pallas kernels for 0% -> 0%
where the time goes in v1:
time: 417 us
  waiting for transfers between devices  214 us (51%)
  blocking collectives  140 us (34%)
  matrix products  44.3 us (11%)
  between operations  13.8 us (3%)
  local copies, waits for them, and re-layouts  4.35 us (1%)
    all_to_all x1, blocking collectives, shards(): lax.all_to_all(basis_vectors, 'row', split_axis=0, concat_axis=0, tiled=T...  109 us
    reduce_scatter x1, waiting for transfers between devices, shards(): lax.psum_scatter(partial_proj, 'row', scatter_dimension=0, tiled=True)  81.6 us
    all_gather x1, waiting for transfers between devices, shards(): own = lax.all_gather(basis_vectors, ('col', 'sub'), axis=1, tiled=True)  62.6 us
    reduce_scatter x1, waiting for transfers between devices, shards(): image = lax.psum_scatter(part, 'row', scatter_dimension=0, tiled=True)  42.5 us
    dot_general x1, matrix products, shards(): lax.dot_general(matrix, own, (((0,), (0,)), ((), ())), precision=lax.Prec...  33.4 us
    all_to_all x1, blocking collectives, shards(): lax.all_to_all(spread, ('col', 'sub'), split_axis=0, concat_axis=1, tiled...  28.1 us
    reduce_scatter x1, waiting for transfers between devices, shards(): lax.psum_scatter(proj, ('col', 'sub'), scatter_dimension=1, tiled=True)  27 us
    dot_general x1, matrix products, shards(): lax.dot_general(mine, image, (((0,), (0,)), ((), ())), precision=lax.Prec...  10.8 us
  transfers between devices with their start and end apart: 4, of which 4 were waited for; matrix products, arithmetic and copies ran while one was open for 0% of the time, Pallas kernels for 0%

profile of v1, /device:TPU:0, one launch (start us, length us, event | category | flops | bytes accessed | tf_op | source)
XLA Modules:
  0.0 417.1 jit_solution(6435462178155145965)
XLA Ops:
  6.5 0.0 all-gather.2.cloned.1.call-start
  6.5 0.7 all-gather.2.cloned.1.call-update
  7.3 0.0 reduce-scatter.4.cloned.1.call-start
  7.3 62.6 %all-gather.2.cloned.1.call-done = f32[2048,1024]{1,0:T(8,128)} async-done(((f32[2048,256]{1,0:T(8,128)}), f32[2048,1024]{1,0:T(8,128)}) %all-gather.2.cloned.1.call-update) | async-done | bytes 8388624 | tf_op jit(solution)/shard_map/all_gather | solution.py:18
  69.9 33.4 %fusion.2 = f32[2048,1024]{1,0:T(8,128)} fusion(f32[2048,2048]{1,0:T(8,128)} %param.3, f32[2048,1024]{1,0:T(8,128)} %all-gather.2.cloned.1.call-done), kind=kOutput, calls=%fused_computation.6 | convolution fusion | flops 25769803776 | bytes 33554432 | tf_op jit(solution)/shard_map/dot_general | solution.py:19
  103.3 0.0 copy-start
  103.3 0.0 reduce-scatter.4.cloned.1.call-update
  103.4 0.0 reduce-scatter.6.cloned.1.call-start
  103.4 1.5 copy-done
  104.9 109.4 %all_to_all.25 = f32[4,512,256]{2,1,0:T(8,128)S(1)} all-to-all(f32[4,512,256]{2,1,0:T(8,128)S(1)} %bitcast.14), channel_id=1, replica_groups=mesh['groups'=2,'row'=4,'col'=2,'sub'=2] {'row'}, dimensions={0} | all-to-all | bytes 4194304 | tf_op jit(solution)/shard_map/all_to_all | solution.py:16
  214.3 28.1 %all_to_all.26 = f32[4,512,256]{2,1,0:T(8,128)S(1)} all-to-all(f32[4,512,256]{2,1,0:T(8,128)S(1)} %all_to_all.25), channel_id=1, replica_groups=mesh['groups'=2,'row'=4,'col'=2,'sub'=2] {'col','sub'}, dimensions={0} | all-to-all | bytes 4194304 | tf_op jit(solution)/shard_map/all_to_all | solution.py:17
  242.4 1.8 copy.6
  244.3 42.5 %reduce-scatter.4.cloned.1.call-done = f32[512,1024]{1,0:T(8,128)} async-done(((f32[2048,1024]{1,0:T(8,128)}), f32[512,1024]{1,0:T(8,128)}) %reduce-scatter.4.cloned.1.call-update) | async-done | bytes 2097168 | tf_op jit(solution)/shard_map/reduce_scatter | solution.py:27
  286.8 10.8 %convolution_bitcast_fusion = f32[1024,1024]{0,1:T(8,128)} fusion(f32[512,1024]{1,0:T(8,128)} %reduce-scatter.4.cloned.1.call-done, f32[512,1024]{0,1:T(8,128)} %bitcast.16), kind=kOutput, calls=%fused_computation | convolution fusion | flops 3221225472 | bytes 8388608 | tf_op jit(solution)/shard_map/dot_general | solution.py:28
  297.6 0.0 reduce-scatter.6.cloned.1.call-update
  297.6 0.0 reduce-scatter.8.cloned.1.call-start
  297.7 81.6 %reduce-scatter.6.cloned.1.call-done = f32[256,1024]{0,1:T(8,128)} async-done(((f32[1024,1024]{0,1:T(8,128)}), f32[256,1024]{0,1:T(8,128)}) %reduce-scatter.6.cloned.1.call-update) | async-done | bytes 1048592 | tf_op jit(solution)/shard_map/reduce_scatter | solution.py:35
  379.3 0.0 reduce-scatter.8.cloned.1.call-update
  380.0 27.0 %reduce-scatter.8.cloned.1.call-done = f32[256,256]{0,1:T(8,128)} async-done(((f32[256,1024]{0,1:T(8,128)}), f32[256,256]{0,1:T(8,128)}) %reduce-scatter.8.cloned.1.call-update) | async-done | bytes 262160 | tf_op jit(solution)/shard_map/reduce_scatter | solution.py:36
  407.0 2.4 all_gather.7
  409.4 0.2 select_bitcast_fusion
  409.6 1.0 copy.7
  (2 shorter events, 0.0 us)
Async XLA Ops:
  6.5 63.4 %all-gather.2.cloned.1.call-start = ((), (), s32[]{:S(2)}) async-start(), calls=%async_computation.5 | async-start | bytes 10485760 | tf_op jit(solution)/shard_map/all_gather | solution.py:18
  7.3 279.5 %reduce-scatter.4.cloned.1.call-start = ((), (), s32[]{:S(2)}) async-start(), calls=%async_computation.6 | async-start | bytes 10485760 | tf_op jit(solution)/shard_map/reduce_scatter | solution.py:27
  103.3 1.6 copy-start
  103.4 275.9 %reduce-scatter.6.cloned.1.call-start = ((), (), s32[]{:S(2)}) async-start(), calls=%async_computation.7 | async-start | bytes 5242880 | tf_op jit(solution)/shard_map/reduce_scatter | solution.py:35
  297.6 109.3 %reduce-scatter.8.cloned.1.call-start = ((), (), s32[]{:S(2)}) async-start(), calls=%async_computation.8 | async-start | bytes 1310720 | tf_op jit(solution)/shard_map/reduce_scatter | solution.py:36
Sparse Core Ops, SparseCore 0:
  8.9 60.9 all-gather.1
  103.5 183.2 reduce-scatter.3
  297.8 81.4 reduce-scatter.5
  381.7 25.2 reduce-scatter.7

commit v2 on v1

--- a/solution.py
+++ b/solution.py
@@ -1,7 +1,135 @@
+import functools
+
 import jax
 import jax.numpy as jnp
 from jax import lax
+from jax.experimental import pallas as pl
+from jax.experimental.pallas import tpu as pltpu
 from jax.sharding import PartitionSpec as P
+
+MESH = pl.DeviceIdType.MESH
+CHUNKS = 2
+
+
+def gather_kernel(R, X, S, v, own, spread, lsem, xs, xr, zs, zr, ps, pr, fs, fr):
+    r, x, s = lax.axis_index("row"), lax.axis_index("col"), lax.axis_index("sub")
+    m, kd = v.shape
+    piece = m // R
+
+    def columns(cx, cs):
+        return pl.ds(pl.multiple_of((cx * S + cs) * kd, kd), kd)
+
+    peers = [{"col": lax.rem(x + d, X)} for d in range(1, X)]
+    peers += [{"row": lax.rem(r + d, R)} for d in range(1, R)]
+    peers += [{"sub": lax.rem(s + d, S)} for d in range(1, S)]
+    barrier = pltpu.get_barrier_semaphore()
+    for peer in peers:
+        pl.semaphore_signal(barrier, inc=1, device_id=peer, device_id_type=MESH)
+    pl.semaphore_wait(barrier, len(peers))
+
+    mine = own.at[:, columns(x, s)]
+    across, spreads, partner, forward = [], [], [], []
+    for d in range(1, X):
+        across.append(pltpu.make_async_remote_copy(
+            v, mine, xs.at[d - 1], xr.at[d - 1],
+            device_id={"col": lax.rem(x + d, X)}, device_id_type=MESH))
+    for d in range(1, R):
+        i = lax.rem(r + d, R)
+        spreads.append(pltpu.make_async_remote_copy(
+            v.at[pl.ds(pl.multiple_of(i * piece, piece), piece), :], spread.at[r],
+            zs.at[d - 1], zr.at[d - 1],
+            device_id={"row": i}, device_id_type=MESH))
+    for d in range(1, S):
+        partner.append(pltpu.make_async_remote_copy(
+            v, mine, ps.at[d - 1], pr.at[d - 1],
+            device_id={"sub": lax.rem(s + d, S)}, device_id_type=MESH))
+    for copy in across + spreads + partner:
+        copy.start()
+    local = [
+        pltpu.make_async_copy(v, mine, lsem.at[0]),
+        pltpu.make_async_copy(
+            v.at[pl.ds(pl.multiple_of(r * piece, piece), piece), :], spread.at[r], lsem.at[1]),
+    ]
+    for copy in local:
+        copy.start()
+    for d in range(1, X):
+        across[d - 1].wait_recv()
+        block = own.at[:, columns(lax.rem(x - d + X, X), s)]
+        for e in range(1, S):
+            copy = pltpu.make_async_remote_copy(
+                block, block, fs.at[d - 1, e - 1], fr.at[d - 1, e - 1],
+                device_id={"sub": lax.rem(s + e, S)}, device_id_type=MESH)
+            copy.start()
+            forward.append(copy)
+    for copy in across:
+        copy.wait_send()
+    for copy in spreads + partner + forward:
+        copy.wait()
+    for copy in local:
+        copy.wait()
+
+
+def gather(v, R, X, S):
+    m, kd = v.shape
+    dma = pltpu.SemaphoreType.DMA
+    return pl.pallas_call(
+        functools.partial(gather_kernel, R, X, S),
+        out_shape=(
+            jax.ShapeDtypeStruct((m, kd * X * S), v.dtype),
+            jax.ShapeDtypeStruct((R, m // R, kd), v.dtype),
+        ),
+        in_specs=[pl.BlockSpec(memory_space=pltpu.VMEM)],
+        out_specs=(pl.BlockSpec(memory_space=pl.ANY), pl.BlockSpec(memory_space=pl.ANY)),
+        scratch_shapes=[
+            dma((2,)), dma((X - 1,)), dma((X - 1,)), dma((R - 1,)), dma((R - 1,)),
+            dma((S - 1,)), dma((S - 1,)), dma((X - 1, S - 1)), dma((X - 1, S - 1)),
+        ],
+        compiler_params=pltpu.CompilerParams(collective_id=0, has_side_effects=True),
+        cost_estimate=pl.CostEstimate(flops=0, bytes_accessed=100_000_000, transcendentals=0),
+        name="gather",
+    )(v)
+
+
+def regroup_kernel(X, S, spread, mine, lsem, ss, rs):
+    x, s = lax.axis_index("col"), lax.axis_index("sub")
+    C = X * S
+    k = x * S + s
+    R, piece, kd = spread.shape
+    per = R // C
+    barrier = pltpu.get_barrier_semaphore()
+    dests = [lax.rem(k + e, C) for e in range(C)]
+    for j in dests[1:]:
+        pl.semaphore_signal(
+            barrier, inc=1, device_id={"col": j // S, "sub": lax.rem(j, S)}, device_id_type=MESH)
+    pl.semaphore_wait(barrier, C - 1)
+    target = mine.at[:, :, pl.ds(pl.multiple_of(k * kd, kd), kd)]
+    copies = []
+    for e in range(1, C):
+        j = dests[e]
+        copies.append(pltpu.make_async_remote_copy(
+            spread.at[pl.ds(j * per, per)], target, ss.at[e - 1], rs.at[e - 1],
+            device_id={"col": j // S, "sub": lax.rem(j, S)}, device_id_type=MESH))
+    copies.append(pltpu.make_async_copy(spread.at[pl.ds(k * per, per)], target, lsem))
+    for copy in copies:
+        copy.start()
+    for copy in copies:
+        copy.wait()
+
+
+def regroup(spread, X, S):
+    R, piece, kd = spread.shape
+    C = X * S
+    dma = pltpu.SemaphoreType.DMA
+    return pl.pallas_call(
+        functools.partial(regroup_kernel, X, S),
+        out_shape=jax.ShapeDtypeStruct((R // C, piece, kd * C), spread.dtype),
+        in_specs=[pl.BlockSpec(memory_space=pltpu.VMEM)],
+        out_specs=pl.BlockSpec(memory_space=pl.ANY),
+        scratch_shapes=[dma, dma((C - 1,)), dma((C - 1,))],
+        compiler_params=pltpu.CompilerParams(collective_id=1, has_side_effects=True),
+        cost_estimate=pl.CostEstimate(flops=0, bytes_accessed=60_000_000, transcendentals=0),
+        name="regroup",
+    )(spread)
 
 
 def shards(matrix, basis_vectors, split_size):
@@ -13,24 +141,34 @@
     n = matrix.shape[1]
     per = n // m
     piece = m // R
-    spread = lax.all_to_all(basis_vectors, "row", split_axis=0, concat_axis=0, tiled=True)
-    mine = lax.all_to_all(spread, ("col", "sub"), split_axis=0, concat_axis=1, tiled=True)
-    own = lax.all_gather(basis_vectors, ("col", "sub"), axis=1, tiled=True)
-    part = lax.dot_general(
-        matrix,
-        own,
-        (((0,), (0,)), ((), ())),
-        precision=lax.Precision.HIGH,
-        preferred_element_type=jnp.float32,
-    )
-    part = part.reshape(per, R, piece, K).transpose(1, 0, 2, 3).reshape(R * per * piece, K)
-    image = lax.psum_scatter(part, "row", scatter_dimension=0, tiled=True)
-    partial_proj = lax.dot_general(
-        mine,
-        image,
-        (((0,), (0,)), ((), ())),
-        precision=lax.Precision.HIGH,
-        preferred_element_type=jnp.float32,
+    own, spread = gather(basis_vectors, R, C // S, S)
+    width = K // CHUNKS
+    images = []
+    for c in range(CHUNKS):
+        part = lax.dot_general(
+            matrix,
+            own[:, c * width : (c + 1) * width],
+            (((0,), (0,)), ((), ())),
+            precision=lax.Precision.HIGH,
+            preferred_element_type=jnp.float32,
+        )
+        if c == 0:
+            part, spread = lax.optimization_barrier((part, spread))
+        part = part.reshape(per, R, piece, width).transpose(1, 0, 2, 3).reshape(R * per * piece, width)
+        images.append(lax.psum_scatter(part, "row", scatter_dimension=0, tiled=True))
+    mine = regroup(spread, C // S, S).reshape(per * piece, K)
+    partial_proj = jnp.concatenate(
+        [
+            lax.dot_general(
+                mine,
+                image,
+                (((0,), (0,)), ((), ())),
+                precision=lax.Precision.HIGH,
+                preferred_element_type=jnp.float32,
+            )
+            for image in images
+        ],
+        axis=1,
     )
     proj = lax.psum_scatter(partial_proj, "row", scatter_dimension=0, tiled=True)
     proj = lax.psum_scatter(proj, ("col", "sub"), scatter_dimension=1, tiled=True)

time: 417 us -> 359 us (0.86)
  blocking collectives: 140 us -> 2.38 us
  Pallas kernels: 0 us -> 83.1 us
    all_to_all x2 -> x0, blocking collectives: 137 us -> none  [the longest x1 109 us: shards(): lax.all_to_all(basis_vectors, 'row', split_axis=0, concat_axis=0, tiled=T...]
    pallas_call x0 -> x2, Pallas kernels: none -> 83.1 us  [the longest x1 57.9 us: gather(): pl.pallas_call(functools.partial(gather_kernel, R, X, S), out_shape=(jax....]
    reduce_scatter x1 -> x2, waiting for transfers between devices: 42.5 us -> 106 us  [shards(): lax.psum_scatter(part, 'row', scatter_dimension=0, tiled=True)]
    all_gather x1 -> x0, waiting for transfers between devices: 62.6 us -> none  [shards(): own = lax.all_gather(basis_vectors, ('col', 'sub'), axis=1, tiled=True)]
    reduce_scatter x1, waiting for transfers between devices: 81.6 us -> 77.4 us  [shards(): lax.psum_scatter(partial_proj, 'row', scatter_dimension=0, tiled=True)]
    dot_general x1 -> x2, matrix products: 33.4 us -> 36.7 us  [shards(): lax.dot_general(matrix, own[:, c * width:(c + 1) * width], (((0,), (0,)),...]
    dot_general x1 -> x2, matrix products: 10.8 us -> 8.23 us  [shards(): lax.dot_general(mine, image, (((0,), (0,)), ((), ())), precision=lax.Prec...]
  transfers between devices with their start and end apart: 4 -> 4, of which waited for: 4 -> 4; matrix products, arithmetic and copies ran while one was open for 0% -> 7% of each run, Pallas kernels for 0% -> 7%
where the time goes in v2:
time: 359 us
  waiting for transfers between devices  210 us (58%)
  Pallas kernels  83.1 us (23%)
  matrix products  45 us (13%)
  between operations  13.8 us (4%)
    reduce_scatter x2, waiting for transfers between devices, shards(): lax.psum_scatter(part, 'row', scatter_dimension=0, tiled=True)  106 us
    reduce_scatter x1, waiting for transfers between devices, shards(): lax.psum_scatter(partial_proj, 'row', scatter_dimension=0, tiled=True)  77.4 us
    pallas_call x1, Pallas kernels, gather(): pl.pallas_call(functools.partial(gather_kernel, R, X, S), out_shape=(jax....  57.9 us
    dot_general x2, matrix products, shards(): lax.dot_general(matrix, own[:, c * width:(c + 1) * width], (((0,), (0,)),...  36.7 us
    reduce_scatter x1, waiting for transfers between devices, shards(): lax.psum_scatter(proj, ('col', 'sub'), scatter_dimension=1, tiled=True)  27 us
    pallas_call x1, Pallas kernels, regroup(): pl.pallas_call(functools.partial(regroup_kernel, X, S), out_shape=jax.Sha...  25.2 us
    dot_general x2, matrix products, shards(): lax.dot_general(mine, image, (((0,), (0,)), ((), ())), precision=lax.Prec...  8.23 us
  transfers between devices with their start and end apart: 4, of which 4 were waited for; matrix products, arithmetic and copies ran while one was open for 7% of the time, Pallas kernels for 7%

profile of v2, /device:TPU:0, one launch (start us, length us, event | category | flops | bytes accessed | tf_op | source)
XLA Modules:
  0.0 358.6 jit_solution(15398420941739360031)
XLA Ops:
  6.5 0.0 reduce-scatter.7.cloned.1.call-start
  6.5 57.9 %gather.1 = (f32[2048,1024]{1,0:T(8,128)}, f32[4,512,256]{2,1,0:T(8,128)}) custom-call(f32[2048,256]{1,0:T(8,128)} %v.1), custom_call_target="tpu_custom_call" | custom-call | bytes 100000000 | tf_op jit(solution)/shard_map/gather/pallas_call | solution.py:75
  64.4 18.4 %fusion = f32[2048,512]{1,0:T(8,128)} fusion(f32[2048,2048]{1,0:T(8,128)} %param.3, f32[2048,1024]{1,0:T(8,128)} %get-tuple-element.9), kind=kOutput, calls=%fused_computation.1 | convolution fusion | flops 12884901888 | bytes 25165824 | tf_op jit(solution)/shard_map/dot_general | solution.py:148
  82.8 0.0 reduce-scatter.7.cloned.1.call-update
  82.8 0.0 reduce-scatter.5.cloned.1.call-start
  82.8 18.4 %fusion.2 = f32[2048,512]{1,0:T(8,128)} fusion(f32[2048,2048]{1,0:T(8,128)} %param.3, f32[2048,1024]{1,0:T(8,128)} %get-tuple-element.9), kind=kOutput, calls=%fused_computation.3 | convolution fusion | flops 12884901888 | bytes 25165824 | tf_op jit(solution)/shard_map/dot_general | solution.py:148
  101.2 0.0 reduce-scatter.5.cloned.1.call-update
  101.2 0.2 reduce-scatter.9.cloned.1.call-start
  101.5 25.2 %regroup.1 = f32[1,512,1024]{2,1,0:T(8,128)} custom-call(f32[4,512,256]{2,1,0:T(8,128)} %get-tuple-element.11.spread), custom_call_target="tpu_custom_call" | custom-call | bytes 60000000 | tf_op jit(solution)/shard_map/regroup/pallas_call | solution.py:123
  126.7 0.0 copy-start
  126.7 31.2 %reduce-scatter.7.cloned.1.call-done = f32[512,512]{1,0:T(8,128)} async-done(((f32[2048,512]{1,0:T(8,128)}), f32[512,512]{1,0:T(8,128)}) %reduce-scatter.7.cloned.1.call-update) | async-done | bytes 1048592 | tf_op jit(solution)/shard_map/reduce_scatter | solution.py:158
  157.9 5.0 %fusion.4 = f32[1024,512]{0,1:T(8,128)} fusion(f32[512,512]{1,0:T(8,128)} %reduce-scatter.7.cloned.1.call-done, f32[1,512,1024]{2,1,0:T(8,128)} %regroup.1), kind=kOutput, calls=%fused_computation.5 | convolution fusion | flops 1610612736 | bytes 5242880 | tf_op jit(solution)/shard_map/dot_general | solution.py:162
  162.9 74.7 %reduce-scatter.5.cloned.1.call-done = f32[512,512]{1,0:T(8,128)} async-done(((f32[2048,512]{1,0:T(8,128)}), f32[512,512]{1,0:T(8,128)}) %reduce-scatter.5.cloned.1.call-update) | async-done | bytes 1048592 | tf_op jit(solution)/shard_map/reduce_scatter | solution.py:158
  237.6 0.0 copy-done
  237.6 0.0 copy-start.1
  237.6 3.2 fusion.6
  240.8 0.0 copy-done.1
  240.8 2.5 pad_maximum_fusion
  243.3 0.0 reduce-scatter.9.cloned.1.call-update
  243.3 0.0 reduce-scatter.11.cloned.1.call-start
  243.4 77.4 %reduce-scatter.9.cloned.1.call-done = f32[256,1024]{0,1:T(8,128)} async-done(((f32[1024,1024]{0,1:T(8,128)}), f32[256,1024]{0,1:T(8,128)}) %reduce-scatter.9.cloned.1.call-update) | async-done | bytes 1048592 | tf_op jit(solution)/shard_map/reduce_scatter | solution.py:173
  320.8 0.0 reduce-scatter.11.cloned.1.call-update
  321.5 27.0 %reduce-scatter.11.cloned.1.call-done = f32[256,256]{0,1:T(8,128)} async-done(((f32[256,1024]{0,1:T(8,128)}), f32[256,256]{0,1:T(8,128)}) %reduce-scatter.11.cloned.1.call-update) | async-done | bytes 262160 | tf_op jit(solution)/shard_map/reduce_scatter | solution.py:174
  348.5 2.4 all_gather.3
  350.8 0.2 select_bitcast_fusion
  351.1 1.0 copy.4
  (2 shorter events, 0.0 us)
Async XLA Ops:
  6.5 151.4 %reduce-scatter.7.cloned.1.call-start = ((), (), s32[]{:S(2)}) async-start(), calls=%async_computation.5 | async-start | bytes 5242880 | tf_op jit(solution)/shard_map/reduce_scatter | solution.py:158
  82.8 154.8 %reduce-scatter.5.cloned.1.call-start = ((), (), s32[]{:S(2)}) async-start(), calls=%async_computation.4 | async-start | bytes 5242880 | tf_op jit(solution)/shard_map/reduce_scatter | solution.py:158
  101.2 219.5 %reduce-scatter.9.cloned.1.call-start = ((), (), s32[]{:S(2)}) async-start(), calls=%async_computation.6 | async-start | bytes 5242880 | tf_op jit(solution)/shard_map/reduce_scatter | solution.py:173
  126.7 110.9 %copy-start = (f32[1,512,1024]{2,1,0:T(8,128)S(1)}, f32[1,512,1024]{2,1,0:T(8,128)}, u32[]{:S(2)}) copy-start(f32[1,512,1024]{2,1,0:T(8,128)} %regroup.1) | copy-start | bytes 6291460
  237.6 3.2 copy-start.1
  243.3 105.1 %reduce-scatter.11.cloned.1.call-start = ((), (), s32[]{:S(2)}) async-start(), calls=%async_computation.7 | async-start | bytes 1310720 | tf_op jit(solution)/shard_map/reduce_scatter | solution.py:174
Sparse Core Ops, SparseCore 0:
  82.9 74.9 reduce-scatter.6
  160.2 77.3 reduce-scatter.4
  243.4 77.2 reduce-scatter.8
  323.2 25.2 reduce-scatter.10

commit v3 on v2

--- a/solution.py
+++ b/solution.py
@@ -8,7 +8,7 @@
 from jax.sharding import PartitionSpec as P
 
 MESH = pl.DeviceIdType.MESH
-CHUNKS = 2
+CHUNKS = 1
 
 
 def gather_kernel(R, X, S, v, own, spread, lsem, xs, xr, zs, zr, ps, pr, fs, fr):
@@ -132,6 +132,116 @@
     )(spread)
 
 
+def project_kernel(R, X, S, p, out, acc, from_sub, from_col, from_row, res, from_pair,
+                   a_s, a_r, b_s, b_r, c_s, c_r, d_s, d_r):
+    r, x, s = lax.axis_index("row"), lax.axis_index("col"), lax.axis_index("sub")
+    K = p.shape[0]
+    rb, kd = K // R, K // (X * S)
+
+    def rows(i):
+        return pl.ds(pl.multiple_of(i * rb, rb), rb)
+
+    def columns(cx, cs):
+        return pl.ds(pl.multiple_of((cx * S + cs) * kd, kd), kd)
+
+    def col(d):
+        return lax.rem(x + d, X)
+
+    peers = [{"col": col(d)} for d in range(1, X)]
+    peers += [{"row": lax.rem(r + d, R)} for d in range(1, R)]
+    peers += [{"sub": lax.rem(s + d, S)} for d in range(1, S)]
+    barrier = pltpu.get_barrier_semaphore()
+    for peer in peers:
+        pl.semaphore_signal(barrier, inc=1, device_id=peer, device_id_type=MESH)
+    pl.semaphore_wait(barrier, len(peers))
+
+    order = list(range(1, X)) + [0]
+    steps = list(range(1, R)) + [0]
+    pair = {}
+    for d in order:
+        for e in range(1, S):
+            other = lax.rem(s + e, S)
+            pair[d, e] = pltpu.make_async_remote_copy(
+                p.at[:, columns(col(d), other)], from_sub.at[e - 1, d],
+                a_s.at[e - 1, d], a_r.at[e - 1, d],
+                device_id={"sub": other}, device_id_type=MESH)
+            pair[d, e].start()
+    cross = {}
+    for d in order:
+        for e in range(1, S):
+            pair[d, e].wait_recv()
+        for q in steps:
+            here = rows(lax.rem(r + q, R))
+            total = p[here, columns(col(d), s)]
+            for e in range(1, S):
+                total = total + from_sub[e - 1, d, here, :]
+            acc[d, here, :] = total
+            if d > 0:
+                cross[d, q] = pltpu.make_async_remote_copy(
+                    acc.at[d, here], from_col.at[d - 1, here],
+                    b_s.at[d - 1, q], b_r.at[d - 1, q],
+                    device_id={"col": col(d)}, device_id_type=MESH)
+                cross[d, q].start()
+    along = []
+    for q in steps:
+        i = lax.rem(r + q, R)
+        here = rows(i)
+        total = acc[0, here, :]
+        for d in range(1, X):
+            cross[d, q].wait_recv()
+            total = total + from_col[d - 1, here, :]
+        if q > 0:
+            acc[0, here, :] = total
+            copy = pltpu.make_async_remote_copy(
+                acc.at[0, here], from_row.at[q - 1], c_s.at[q - 1], c_r.at[q - 1],
+                device_id={"row": i}, device_id_type=MESH)
+            copy.start()
+            along.append(copy)
+    for q in range(1, R):
+        along[q - 1].wait_recv()
+        total = total + from_row[q - 1]
+    res[...] = total
+    last = []
+    for e in range(1, S):
+        copy = pltpu.make_async_remote_copy(
+            res, from_pair.at[e - 1], d_s.at[e - 1], d_r.at[e - 1],
+            device_id={"sub": lax.rem(s + e, S)}, device_id_type=MESH)
+        copy.start()
+        last.append(copy)
+    out[:, pl.ds(pl.multiple_of(s * kd, kd), kd)] = total
+    for e in range(1, S):
+        last[e - 1].wait_recv()
+        out[:, pl.ds(pl.multiple_of(lax.rem(s - e + S, S) * kd, kd), kd)] = from_pair[e - 1]
+    for copy in list(pair.values()) + list(cross.values()) + along + last:
+        copy.wait_send()
+
+
+def project(partial, R, X, S):
+    K = partial.shape[0]
+    rb, kd = K // R, K // (X * S)
+    dma = pltpu.SemaphoreType.DMA
+    f32 = jnp.float32
+    return pl.pallas_call(
+        functools.partial(project_kernel, R, X, S),
+        out_shape=jax.ShapeDtypeStruct((rb, S * kd), f32),
+        in_specs=[pl.BlockSpec(memory_space=pltpu.VMEM)],
+        out_specs=pl.BlockSpec(memory_space=pltpu.VMEM),
+        scratch_shapes=[
+            pltpu.VMEM((X, K, kd), f32),
+            pltpu.VMEM((S - 1, X, K, kd), f32),
+            pltpu.VMEM((X - 1, K, kd), f32),
+            pltpu.VMEM((R - 1, rb, kd), f32),
+            pltpu.VMEM((rb, kd), f32),
+            pltpu.VMEM((S - 1, rb, kd), f32),
+            dma((S - 1, X)), dma((S - 1, X)), dma((X - 1, R)), dma((X - 1, R)),
+            dma((R - 1,)), dma((R - 1,)), dma((S - 1,)), dma((S - 1,)),
+        ],
+        compiler_params=pltpu.CompilerParams(collective_id=2, has_side_effects=True),
+        cost_estimate=pl.CostEstimate(flops=0, bytes_accessed=60_000_000, transcendentals=0),
+        name="project",
+    )(partial)
+
+
 def shards(matrix, basis_vectors, split_size):
     R = lax.axis_size("row")
     S = lax.axis_size("sub")
@@ -170,9 +280,7 @@
         ],
         axis=1,
     )
-    proj = lax.psum_scatter(partial_proj, "row", scatter_dimension=0, tiled=True)
-    proj = lax.psum_scatter(proj, ("col", "sub"), scatter_dimension=1, tiled=True)
-    child_block = lax.all_gather(proj, "sub", axis=1, tiled=True)
+    child_block = project(partial_proj, R, C // S, S)
     row_ids = (
         jnp.arange(child_block.shape[0], dtype=jnp.int32)
         + lax.axis_index("row") * child_block.shape[0]

time: 359 us -> 299 us (0.83)
  waiting for transfers between devices: 210 us -> 117 us
  Pallas kernels: 83.1 us -> 125 us
  matrix products: 45 us -> 41.1 us
    reduce_scatter x2 -> x0, waiting for transfers between devices: 104 us -> none  [the longest x1 77.4 us: shards(): lax.psum_scatter(partial_proj, 'row', scatter_dimension=0, tiled=True)]
    pallas_call x0 -> x1, Pallas kernels: none -> 41.8 us  [project(): pl.pallas_call(functools.partial(project_kernel, R, X, S), out_shape=jax....]
    reduce_scatter x2 -> x1, waiting for transfers between devices: 106 us -> 117 us  [shards(): lax.psum_scatter(part, 'row', scatter_dimension=0, tiled=True)]
    dot_general x2 -> x1, matrix products: 36.7 us -> 33.4 us  [shards(): lax.dot_general(matrix, own[:, c * width:(c + 1) * width], (((0,), (0,)),...]
    dot_general x2 -> x1, matrix products: 8.23 us -> 7.69 us  [shards(): lax.dot_general(mine, image, (((0,), (0,)), ((), ())), precision=lax.Prec...]
  transfers between devices with their start and end apart: 4 -> 1, of which waited for: 4 -> 1; matrix products, arithmetic and copies ran while one was open for 7% -> 0% of each run, Pallas kernels for 7% -> 8%
where the time goes in v3:
time: 299 us
  Pallas kernels  125 us (42%)
  waiting for transfers between devices  117 us (39%)
  matrix products  41.1 us (14%)
  between operations  14.1 us (5%)
    reduce_scatter x1, waiting for transfers between devices, shards(): lax.psum_scatter(part, 'row', scatter_dimension=0, tiled=True)  117 us
    pallas_call x1, Pallas kernels, gather(): pl.pallas_call(functools.partial(gather_kernel, R, X, S), out_shape=(jax....  57.9 us
    pallas_call x1, Pallas kernels, project(): pl.pallas_call(functools.partial(project_kernel, R, X, S), out_shape=jax....  41.8 us
    dot_general x1, matrix products, shards(): lax.dot_general(matrix, own[:, c * width:(c + 1) * width], (((0,), (0,)),...  33.4 us
    pallas_call x1, Pallas kernels, regroup(): pl.pallas_call(functools.partial(regroup_kernel, X, S), out_shape=jax.Sha...  25.2 us
    dot_general x1, matrix products, shards(): lax.dot_general(mine, image, (((0,), (0,)), ((), ())), precision=lax.Prec...  7.69 us
  transfers between devices with their start and end apart: 1, of which 1 were waited for; matrix products, arithmetic and copies ran while one was open for 0% of the time, Pallas kernels for 8%

profile of v3, /device:TPU:0, one launch (start us, length us, event | category | flops | bytes accessed | tf_op | source)
XLA Modules:
  0.0 299.2 jit_solution(3964352810595357344)
XLA Ops:
  6.5 0.0 reduce-scatter.2.cloned.1.call-start
  6.5 57.9 %gather.1 = (f32[2048,1024]{1,0:T(8,128)}, f32[4,512,256]{2,1,0:T(8,128)}) custom-call(f32[2048,256]{1,0:T(8,128)} %v.1), custom_call_target="tpu_custom_call" | custom-call | bytes 100000000 | tf_op jit(solution)/shard_map/gather/pallas_call | solution.py:75
  64.4 33.4 %fusion.4 = f32[2048,1024]{1,0:T(8,128)} fusion(f32[2048,2048]{1,0:T(8,128)} %param.3, f32[2048,1024]{1,0:T(8,128)} %get-tuple-element.9), kind=kOutput, calls=%fused_computation.7 | convolution fusion | flops 25769803776 | bytes 33554432 | tf_op jit(solution)/shard_map/dot_general | solution.py:258
  97.8 0.0 reduce-scatter.2.cloned.1.call-update
  97.9 25.2 %regroup.1 = f32[1,512,1024]{2,1,0:T(8,128)} custom-call(f32[4,512,256]{2,1,0:T(8,128)} %get-tuple-element.11.spread), custom_call_target="tpu_custom_call" | custom-call | bytes 60000000 | tf_op jit(solution)/shard_map/regroup/pallas_call | solution.py:123
  123.8 117.1 %reduce-scatter.2.cloned.1.call-done = f32[512,1024]{1,0:T(8,128)} async-done(((f32[2048,1024]{1,0:T(8,128)}), f32[512,1024]{1,0:T(8,128)}) %reduce-scatter.2.cloned.1.call-update) | async-done | bytes 2097168 | tf_op jit(solution)/shard_map/reduce_scatter | solution.py:268
  240.8 7.7 %fusion.p = f32[1024,1024]{1,0:T(8,128)} fusion(f32[512,1024]{1,0:T(8,128)} %reduce-scatter.2.cloned.1.call-done, f32[1,512,1024]{2,1,0:T(8,128)} %regroup.1), kind=kOutput, calls=%fused_computation | convolution fusion | flops 3221225472 | bytes 8388608 | tf_op jit(solution)/shard_map/dot_general | solution.py:272
  248.5 41.8 %project.1 = f32[256,512]{1,0:T(8,128)} custom-call(f32[1024,1024]{1,0:T(8,128)} %fusion.p), custom_call_target="tpu_custom_call" | custom-call | bytes 60000000 | tf_op jit(solution)/shard_map/project/pallas_call | solution.py:224
  290.3 2.0 select_bitcast_fusion
  (2 shorter events, 0.0 us)
Async XLA Ops:
  6.5 234.3 %reduce-scatter.2.cloned.1.call-start = ((), (), s32[]{:S(2)}) async-start(), calls=%async_computation.1 | async-start | bytes 10485760 | tf_op jit(solution)/shard_map/reduce_scatter | solution.py:268
Sparse Core Ops, SparseCore 0:
  98.0 142.8 reduce-scatter.1
